TPU v7x, 256 devices: a whole 4x4x8 slice. The times are simulated.
256 devices in a mesh: row: 16 (over x, y), col: 16 (over z, core).
Axes of the slice: x: 4, y: 4, z: 8, core: 2. Of those that a mesh axis runs over, the one named last changes fastest.
Arguments:
- values: bfloat16 [8192, 8192], P('row', 'col'), may hold values from 0.0001296997 to 0.12988281
- tile_mask: int32 [64, 64], P('row', 'col'), may hold values 0 or 1
- keep_mask: int32 [64, 64], P('row', 'col'), may hold values 0 or 1
- thr_index: int32 [8192], P('col'), may hold values from 0 to 9
Outputs:
- expanded: bfloat16 [8192, 8192], P('row', 'col')
All inputs are finite; a program needn't handle non-finite values. No bound on the sum of `tile_mask` or of `keep_mask` on one device may be relied on, other than what follows from the above.
Results may differ from a plain program's by a relative error of at most 0.0004.
Values may be sent and summed in bfloat16 or wider, within the bound.
A program may use at most 64 MiB of HBM per device.

v0:
```python
import jax
import jax.numpy as jnp
from jax import lax
from jax.sharding import Mesh
from jax.sharding import PartitionSpec as P

TB = 128
ROW = ("row_0", "row_1")


def over_axes(x, axes):
    for axis in axes:
        x = lax.psum(x, axis)
    return x


def on_device(values, tile_mask, keep_mask, thr_index):
    row_count, col_count = values.shape
    row_tiles = row_count // TB
    col_tiles = col_count // TB
    matrix = (
        values.reshape(row_tiles, TB, col_tiles, TB)
        * tile_mask[:, None, :, None].astype(jnp.bfloat16)
    ).reshape(row_count, col_count)
    kept_cells = jnp.broadcast_to(
        keep_mask[:, None, :, None].astype(jnp.float32), (row_tiles, TB, col_tiles, TB)
    ).reshape(row_count, col_count)
    order_all = row_count * lax.axis_size(ROW)
    thresholds = 0.125 * thr_index.astype(jnp.float32)
    col_panel = lax.all_gather(matrix, ROW, axis=0, tiled=True)
    product = jnp.dot(
        lax.all_gather(matrix, "col", axis=1, tiled=True),
        col_panel,
        preferred_element_type=jnp.float32,
    )
    outputs = []
    for phase_idx in range(col_tiles):
        lo_col = phase_idx * TB
        part_prod = product[:, lo_col : lo_col + TB]
        col_means = over_axes(jnp.sum(part_prod, axis=0), ROW) / order_all
        pruned = (
            jnp.maximum(part_prod - thresholds[lo_col : lo_col + TB] * col_means, 0.0)
            * kept_cells[:, lo_col : lo_col + TB]
        )
        col_totals = over_axes(jnp.sum(pruned, axis=0), ROW) / order_all
        outputs.append(pruned / jnp.maximum(col_totals, 0.1))
    result = jnp.concatenate(outputs, axis=1)
    return result.astype(jnp.bfloat16)


def solution(mesh):
    finer = Mesh(mesh.devices.reshape(4, 4, mesh.shape["col"]), ("row_0", "row_1", "col"))
    placed = (P(ROW, "col"), P(ROW, "col"), P(ROW, "col"), P("col"))
    return jax.shard_map(
        on_device, mesh=finer, in_specs=placed, out_specs=P(ROW, "col"), check_vma=False
    )
```

profile of v0, /device:TPU:2, one launch (start us, length us, event | category | flops | bytes accessed | tf_op | source)
XLA Modules:
  0.0 198.9 jit_solution(1561034129201004434)
XLA Ops:
  6.5 0.0 all-gather.3.cloned.1.call-start
  6.5 0.7 convert_element_type.12
  7.2 0.2 mul.41
  7.4 1.9 bitcast_multiply_fusion
  9.3 0.0 all-gather.3.cloned.1.call-update
  9.4 0.0 all-gather.5.cloned.1.call-start
  9.4 0.7 all-gather.5.cloned.1.call-update
  10.1 0.7 convert_element_type.14
  10.8 0.2 broadcast_in_dim.2
  11.0 0.1 copy.9
  11.1 0.7 convert_multiply_fusion
  11.8 56.5 %all-gather.3.cloned.1.call-done = bf16[512,8192]{1,0:T(8,128)(2,1)} async-done(((bf16[512,512]{1,0:T(8,128)(2,1)}), bf16[512,8192]{1,0:T(8,128)(2,1)}) %all-gather.3.cloned.1.call-update) | async-done | bytes 8388624 | tf_op jit(solution)/shard_map/all_gather | solution.py:32
  68.3 76.8 %all-gather.5.cloned.1.call-done = bf16[8192,512]{1,0:T(8,128)(2,1)} async-done(((bf16[512,512]{1,0:T(8,128)(2,1)}), bf16[8192,512]{1,0:T(8,128)(2,1)}) %all-gather.5.cloned.1.call-update) | async-done | bytes 8388624 | tf_op jit(solution)/shard_map/all_gather | solution.py:30
  145.1 9.4 %fusion.4 = f32[512,512]{1,0:T(8,128)S(1)} fusion(bf16[512,8192]{1,0:T(8,128)(2,1)} %all-gather.3.cloned.1.call-done, bf16[8192,512]{1,0:T(8,128)(2,1)} %all-gather.5.cloned.1.call-done), kind=kOutput, calls=%fused_computation.28 | convolution fusion | flops 4294967296 | bytes 17825792 | tf_op jit(solution)/shard_map/dot_general | solution.py:31
  154.6 0.1 slice_reduce_fusion.3
  154.7 8.6 %all-reduce.3 = (f32[128]{0:T(128)S(1)}, f32[128]{0:T(128)S(1)}, f32[128]{0:T(128)S(1)}, f32[128]{0:T(128)S(1)}) all-reduce(f32[128]{0:T(128)S(1)} %get-tuple-element.9, f32[128]{0:T(128)S(1)} %get-tuple-element.10, f32[128]{0:T(128)S(1)} %get-tuple-element.11, ...), channel_id=1, replica_groups=mesh['row_0'=4,'row_1'=4,'col'=16] {'row_0'}, use_global_device_ids=true, to_apply=%region_1.0 | all-reduce | flops 512 | bytes 4096 | tf_op jit(solution)/shard_map/psum | solution.py:13
  163.3 10.1 %all-reduce.1 = (f32[128]{0:T(128)S(1)}, f32[128]{0:T(128)S(1)}, f32[128]{0:T(128)S(1)}, f32[128]{0:T(128)S(1)}) all-reduce(f32[128]{0:T(128)S(1)} %get-tuple-element.25, f32[128]{0:T(128)S(1)} %get-tuple-element.26, f32[128]{0:T(128)S(1)} %get-tuple-element.27, ...), channel_id=1, replica_groups=mesh['row_0'=4,'row_1'=4,'col'=16] {'row_1'}, use_global_device_ids=true, to_apply=%region_2.0 | all-reduce | flops 512 | bytes 4096 | tf_op jit(solution)/shard_map/psum | solution.py:13
  173.4 0.2 fusion
  173.5 8.6 %all-reduce.2 = (f32[128]{0:T(128)S(1)}, f32[128]{0:T(128)S(1)}, f32[128]{0:T(128)S(1)}, f32[128]{0:T(128)S(1)}) all-reduce(f32[128]{0:T(128)S(1)} %get-tuple-element.6, f32[128]{0:T(128)S(1)} %get-tuple-element.7, f32[128]{0:T(128)S(1)} %get-tuple-element.8, ...), channel_id=1, replica_groups=mesh['row_0'=4,'row_1'=4,'col'=16] {'row_0'}, use_global_device_ids=true, to_apply=%region_22.0 | all-reduce | flops 512 | bytes 4096 | tf_op jit(solution)/shard_map/psum | solution.py:13
  182.1 8.9 %all-reduce = (f32[128]{0:T(128)S(1)}, f32[128]{0:T(128)S(1)}, f32[128]{0:T(128)S(1)}, f32[128]{0:T(128)S(1)}) all-reduce(f32[128]{0:T(128)S(1)} %get-tuple-element.21, f32[128]{0:T(128)S(1)} %get-tuple-element.22, f32[128]{0:T(128)S(1)} %get-tuple-element.23, ...), channel_id=1, replica_groups=mesh['row_0'=4,'row_1'=4,'col'=16] {'row_1'}, use_global_device_ids=true, to_apply=%region_23.0 | all-reduce | flops 512 | bytes 4096 | tf_op jit(solution)/shard_map/psum | solution.py:13
  191.1 0.2 divide_convert_fusion.3
  191.2 0.9 pad_maximum_fusion
  (3 shorter events, 0.0 us)
Async XLA Ops:
  6.5 61.8 %all-gather.3.cloned.1.call-start = ((), (), s32[]{:S(2)}) async-start(), calls=%async_computation | async-start | bytes 8912896 | tf_op jit(solution)/shard_map/all_gather | solution.py:32
  9.4 135.8 %all-gather.5.cloned.1.call-start = ((), (), s32[]{:S(2)}) async-start(), calls=%async_computation.1 | async-start | bytes 8912896 | tf_op jit(solution)/shard_map/all_gather | solution.py:30
Sparse Core Ops, SparseCore 0:
  9.5 58.7 all-gather.2
  70.7 74.3 all-gather.4
where the time goes:
time: 199 us
  waiting for transfers between devices  134 us (67%)
  blocking collectives  36.2 us (18%)
  between operations  13.4 us (7%)
  matrix products  9.44 us (5%)
  other arithmetic  5.27 us (3%)
    all_gather x1, waiting for transfers between devices, on_device(): col_panel = lax.all_gather(matrix, ROW, axis=0, tiled=True)  76.8 us
    all_gather x1, waiting for transfers between devices, on_device(): lax.all_gather(matrix, 'col', axis=1, tiled=True)  56.5 us
    psum x4, blocking collectives, over_axes(): x = lax.psum(x, axis)  36.2 us
    dot_general x1, matrix products, on_device(): jnp.dot(lax.all_gather(matrix, 'col', axis=1, tiled=True), col_panel, pre...  9.44 us
  transfers between devices with their start and end apart: 2, of which 2 were waited for; matrix products, arithmetic and copies ran while one was open for 1% of the time, Pallas kernels for 0%

commit v1 on v0

--- a/solution.py
+++ b/solution.py
@@ -28,11 +28,10 @@
     order_all = row_count * lax.axis_size(ROW)
     thresholds = 0.125 * thr_index.astype(jnp.float32)
     col_panel = lax.all_gather(matrix, ROW, axis=0, tiled=True)
-    product = jnp.dot(
-        lax.all_gather(matrix, "col", axis=1, tiled=True),
-        col_panel,
-        preferred_element_type=jnp.float32,
+    write_records = lambda block_in, mesh_dim: jnp.concatenate(
+        lax.all_to_all(jnp.stack([block_in] * lax.axis_size(mesh_dim)), mesh_dim, 0, 0), 1
     )
+    product = jnp.dot(write_records(matrix, "col"), col_panel, preferred_element_type=jnp.float32)
     outputs = []
     for phase_idx in range(col_tiles):
         lo_col = phase_idx * TB

time: 199 us -> 261 us (1.31)
  waiting for transfers between devices: 134 us -> 184 us
  starting transfers between devices: 0.04 us -> 8.79 us
  local copies, waits for them, and re-layouts: 0.48 us -> 4.74 us
    all_to_all x0 -> x1, waiting for transfers between devices: none -> 183 us  [on_device(): lax.all_to_all(jnp.stack([block_in] * lax.axis_size(mesh_dim)), mesh_dim,...]
    all_gather x1, waiting for transfers between devices: 76.8 us -> 0.01 us  [on_device(): col_panel = lax.all_gather(matrix, ROW, axis=0, tiled=True)]
    all_gather x1 -> x0, waiting for transfers between devices: 56.5 us -> none  [on_device(): lax.all_gather(matrix, 'col', axis=1, tiled=True)]
    all_to_all x0 -> x1, starting transfers between devices: none -> 8.75 us  [on_device(): lax.all_to_all(jnp.stack([block_in] * lax.axis_size(mesh_dim)), mesh_dim,...]
    another operation x0 -> x1, local copies, waits for them, and re-layouts: none -> 4.03 us  [on_device(): jnp.stack([block_in] * lax.axis_size(mesh_dim))]
  transfers between devices with their start and end apart: 2 -> 2, of which waited for: 2 -> 1; matrix products, arithmetic and copies ran while one was open for 1% -> 0% of each run, Pallas kernels for 0% -> 0%
where the time goes in v1:
time: 261 us
  waiting for transfers between devices  184 us (70%)
  blocking collectives  37.2 us (14%)
  between operations  13.5 us (5%)
  matrix products  9.5 us (4%)
  starting transfers between devices  8.79 us (3%)
  local copies, waits for them, and re-layouts  4.74 us (2%)
  other arithmetic  3.11 us (1%)
    all_to_all x1, waiting for transfers between devices, on_device(): lax.all_to_all(jnp.stack([block_in] * lax.axis_size(mesh_dim)), mesh_dim,...  183 us
    psum x4, blocking collectives, over_axes(): x = lax.psum(x, axis)  37.2 us
    dot_general x1, matrix products, on_device(): jnp.dot(write_records(matrix, 'col'), col_panel, preferred_element_type=j...  9.5 us
    all_to_all x1, starting transfers between devices, on_device(): lax.all_to_all(jnp.stack([block_in] * lax.axis_size(mesh_dim)), mesh_dim,...  8.75 us
  transfers between devices with their start and end apart: 2, of which 1 were waited for; matrix products, arithmetic and copies ran while one was open for 0% of the time, Pallas kernels for 0%

profile of v1, /device:TPU:2, one launch (start us, length us, event | category | flops | bytes accessed | tf_op | source)
XLA Modules:
  0.0 260.7 jit_solution(11468512159247498030)
XLA Ops:
  6.5 0.7 convert_element_type.12
  7.2 0.2 mul.43
  7.4 1.1 bitcast_multiply_fusion
  8.5 0.0 copy-start
  8.6 0.2 copy.5
  8.8 4.0 %stack.3 = bf16[16,512,512]{1,2,0:T(8,128)(2,1)} broadcast(bf16[512,512]{0,1:T(8,128)(2,1)S(1)} %copy.5), dimensions={1,2} | broadcast | bytes 8912896 | tf_op jit(solution)/shard_map/stack | solution.py:32
  12.8 0.0 copy-start.1
  12.8 0.0 copy-start.2
  12.8 0.0 copy-done
  12.8 8.8 %all-to-all-start = ((bf16[16,512,512]{1,2,0:T(8,128)(2,1)}), bf16[16,512,512]{1,2,0:T(8,128)(2,1)}, u32[]{:S(2)}, u32[]{:S(2)}) async-start(bf16[16,512,512]{1,2,0:T(8,128)(2,1)} %stack.3), calls=%async_computation | async-start | bytes 16777216 | tf_op jit(solution)/shard_map/all_to_all | solution.py:32
  21.6 0.0 all-gather.2.cloned.1.call-start
  21.6 0.7 all-gather.2.cloned.1.call-update
  22.3 0.0 copy-done.1
  22.3 0.2 broadcast_in_dim.2
  22.5 0.1 copy.10
  22.6 0.0 copy-done.2
  22.6 183.1 %all-to-all-done = bf16[16,512,512]{1,2,0:T(8,128)(2,1)} async-done(((bf16[16,512,512]{1,2,0:T(8,128)(2,1)}), bf16[16,512,512]{1,2,0:T(8,128)(2,1)}, u32[]{:S(2)}, u32[]{:S(2)}) %all-to-all-start) | async-done | bytes 8388640 | tf_op jit(solution)/shard_map/all_to_all | solution.py:32
  205.8 0.0 all-gather.2.cloned.1.call-done
  205.8 9.5 %fusion.4 = f32[512,512]{1,0:T(8,128)S(1)} fusion(bf16[512,8192]{0,1:T(8,128)(2,1)} %bitcast.1, bf16[8192,512]{1,0:T(8,128)(2,1)} %all-gather.2.cloned.1.call-done), kind=kOutput, calls=%fused_computation.28 | convolution fusion | flops 4294967296 | bytes 17825792 | tf_op jit(solution)/shard_map/dot_general | solution.py:34
  215.3 0.1 slice_reduce_fusion.3
  215.4 8.6 %all-reduce.3 = (f32[128]{0:T(128)S(1)}, f32[128]{0:T(128)S(1)}, f32[128]{0:T(128)S(1)}, f32[128]{0:T(128)S(1)}) all-reduce(f32[128]{0:T(128)S(1)} %get-tuple-element.9, f32[128]{0:T(128)S(1)} %get-tuple-element.10, f32[128]{0:T(128)S(1)} %get-tuple-element.11, ...), channel_id=1, replica_groups=mesh['row_0'=4,'row_1'=4,'col'=16] {'row_0'}, use_global_device_ids=true, to_apply=%region_1.0 | all-reduce | flops 512 | bytes 4096 | tf_op jit(solution)/shard_map/psum | solution.py:13
  224.0 10.7 %all-reduce.1 = (f32[128]{0:T(128)S(1)}, f32[128]{0:T(128)S(1)}, f32[128]{0:T(128)S(1)}, f32[128]{0:T(128)S(1)}) all-reduce(f32[128]{0:T(128)S(1)} %get-tuple-element.25, f32[128]{0:T(128)S(1)} %get-tuple-element.26, f32[128]{0:T(128)S(1)} %get-tuple-element.27, ...), channel_id=1, replica_groups=mesh['row_0'=4,'row_1'=4,'col'=16] {'row_1'}, use_global_device_ids=true, to_apply=%region_2.0 | all-reduce | flops 512 | bytes 4096 | tf_op jit(solution)/shard_map/psum | solution.py:13
  234.8 0.2 fusion
  234.9 10.1 %all-reduce.2 = (f32[128]{0:T(128)S(1)}, f32[128]{0:T(128)S(1)}, f32[128]{0:T(128)S(1)}, f32[128]{0:T(128)S(1)}) all-reduce(f32[128]{0:T(128)S(1)} %get-tuple-element.6, f32[128]{0:T(128)S(1)} %get-tuple-element.7, f32[128]{0:T(128)S(1)} %get-tuple-element.8, ...), channel_id=1, replica_groups=mesh['row_0'=4,'row_1'=4,'col'=16] {'row_0'}, use_global_device_ids=true, to_apply=%region_22.0 | all-reduce | flops 512 | bytes 4096 | tf_op jit(solution)/shard_map/psum | solution.py:13
  245.1 7.7 %all-reduce = (f32[128]{0:T(128)S(1)}, f32[128]{0:T(128)S(1)}, f32[128]{0:T(128)S(1)}, f32[128]{0:T(128)S(1)}) all-reduce(f32[128]{0:T(128)S(1)} %get-tuple-element.21, f32[128]{0:T(128)S(1)} %get-tuple-element.22, f32[128]{0:T(128)S(1)} %get-tuple-element.23, ...), channel_id=1, replica_groups=mesh['row_0'=4,'row_1'=4,'col'=16] {'row_1'}, use_global_device_ids=true, to_apply=%region_23.0 | all-reduce | flops 512 | bytes 4096 | tf_op jit(solution)/shard_map/psum | solution.py:13
  252.8 0.2 divide_convert_fusion.3
  253.0 0.9 pad_maximum_fusion
  (5 shorter events, 0.0 us)
Async XLA Ops:
  8.5 4.3 %copy-start = (bf16[512,512]{1,0:T(8,128)(2,1)}, bf16[512,512]{1,0:T(8,128)(2,1)S(1)}, u32[]{:S(2)}) copy-start(bf16[512,512]{1,0:T(8,128)(2,1)S(1)} %bitcast_multiply_fusion) | copy-start | bytes 1572868
  12.8 9.5 %copy-start.1 = (s32[4,4]{1,0:T(4,128)S(1)}, s32[4,4]{1,0:T(4,128)}, u32[]{:S(2)}) copy-start(s32[4,4]{1,0:T(4,128)} %param.6) | copy-start | bytes 196
  12.8 9.8 %copy-start.2 = (s32[512]{0:T(512)S(1)}, s32[512]{0:T(512)}, u32[]{:S(2)}) copy-start(s32[512]{0:T(512)} %param.7) | copy-start | bytes 6148
  12.8 193.0 %all-to-all-start = ((bf16[16,512,512]{1,2,0:T(8,128)(2,1)}), bf16[16,512,512]{1,2,0:T(8,128)(2,1)}, u32[]{:S(2)}, u32[]{:S(2)}) async-start(bf16[16,512,512]{1,2,0:T(8,128)(2,1)} %stack.3), calls=%async_computation | async-start | bytes 16777216 | tf_op jit(solution)/shard_map/all_to_all | solution.py:32
  21.6 184.2 %all-gather.2.cloned.1.call-start = ((), (), s32[]{:S(2)}) async-start(), calls=%async_computation.1 | async-start | bytes 8912896 | tf_op jit(solution)/shard_map/all_gather | solution.py:30
Sparse Core Ops, SparseCore 0:
  24.8 77.3 all-gather.1

commit v2 on v0

--- a/solution.py
+++ b/solution.py
@@ -10,7 +10,8 @@
 
 def over_axes(x, axes):
     for axis in axes:
-        x = lax.psum(x, axis)
+        parts = lax.all_gather(x, axis, axis=0, tiled=False)
+        x = parts.sum(axis=0)
     return x
 
 

time: 199 us -> 292 us (1.47)
  blocking collectives: 36.2 us -> 129 us
    all_gather x0 -> x16, blocking collectives: none -> 129 us  [over_axes(): parts = lax.all_gather(x, axis, axis=0, tiled=False)]
    psum x4 -> x0, blocking collectives: 36.2 us -> none  [over_axes(): x = lax.psum(x, axis)]
where the time goes in v2:
time: 292 us
  waiting for transfers between devices  134 us (46%)
  blocking collectives  129 us (44%)
  between operations  13.5 us (5%)
  matrix products  9.44 us (3%)
  other arithmetic  5.63 us (2%)
    all_gather x16, blocking collectives, over_axes(): parts = lax.all_gather(x, axis, axis=0, tiled=False)  129 us
    all_gather x1, waiting for transfers between devices, on_device(): col_panel = lax.all_gather(matrix, ROW, axis=0, tiled=True)  76.8 us
    all_gather x1, waiting for transfers between devices, on_device(): lax.all_gather(matrix, 'col', axis=1, tiled=True)  56.5 us
    dot_general x1, matrix products, on_device(): jnp.dot(lax.all_gather(matrix, 'col', axis=1, tiled=True), col_panel, pre...  9.44 us
  transfers between devices with their start and end apart: 2, of which 2 were waited for; matrix products, arithmetic and copies ran while one was open for 1% of the time, Pallas kernels for 0%

profile of v2, /device:TPU:2, one launch (start us, length us, event | category | flops | bytes accessed | tf_op | source)
XLA Modules:
  0.0 291.9 jit_solution(15835337287543353605)
XLA Ops:
  6.5 0.0 all-gather.35.cloned.1.call-start
  6.5 0.7 convert_element_type.12
  7.2 0.2 mul.41
  7.4 1.9 bitcast_multiply_fusion
  9.3 0.0 all-gather.35.cloned.1.call-update
  9.4 0.0 all-gather.37.cloned.1.call-start
  9.4 0.7 all-gather.37.cloned.1.call-update
  10.1 0.7 convert_element_type.14
  10.8 0.2 broadcast_in_dim.2
  11.0 0.1 copy.9
  11.1 0.7 convert_multiply_fusion
  11.8 56.5 %all-gather.35.cloned.1.call-done = bf16[512,8192]{1,0:T(8,128)(2,1)} async-done(((bf16[512,512]{1,0:T(8,128)(2,1)}), bf16[512,8192]{1,0:T(8,128)(2,1)}) %all-gather.35.cloned.1.call-update) | async-done | bytes 8388624 | tf_op jit(solution)/shard_map/all_gather | solution.py:33
  68.3 76.8 %all-gather.37.cloned.1.call-done = bf16[8192,512]{1,0:T(8,128)(2,1)} async-done(((bf16[512,512]{1,0:T(8,128)(2,1)}), bf16[8192,512]{1,0:T(8,128)(2,1)}) %all-gather.37.cloned.1.call-update) | async-done | bytes 8388624 | tf_op jit(solution)/shard_map/all_gather | solution.py:31
  145.1 9.4 %fusion.4 = f32[512,512]{1,0:T(8,128)S(1)} fusion(bf16[512,8192]{1,0:T(8,128)(2,1)} %all-gather.35.cloned.1.call-done, bf16[8192,512]{1,0:T(8,128)(2,1)} %all-gather.37.cloned.1.call-done), kind=kOutput, calls=%fused_computation.28 | convolution fusion | flops 4294967296 | bytes 17825792 | tf_op jit(solution)/shard_map/dot_general | solution.py:32
  154.6 0.1 slice_reduce_fusion.3
  154.7 7.8 %all-gather.16 = f32[4,1,128]{2,1,0:T(1,128)S(1)} all-gather(f32[1,1,128]{2,1,0:T(1,128)S(1)} %bitcast.34), channel_id=2, replica_groups=mesh['row_0'=4,'row_1'=4,'col'=16] {'row_0'}, dimensions={0}, use_global_device_ids=true | all-gather | bytes 2560 | tf_op jit(solution)/shard_map/all_gather | solution.py:13
  162.5 9.3 %all-gather.17 = f32[4,1,128]{2,1,0:T(1,128)S(1)} all-gather(f32[1,1,128]{2,1,0:T(1,128)S(1)} %bitcast.35), channel_id=3, replica_groups=mesh['row_0'=4,'row_1'=4,'col'=16] {'row_1'}, dimensions={0}, use_global_device_ids=true | all-gather | bytes 2560 | tf_op jit(solution)/shard_map/all_gather | solution.py:13
  171.9 7.8 %all-gather.20 = f32[4,1,128]{2,1,0:T(1,128)S(1)} all-gather(f32[1,1,128]{2,1,0:T(1,128)S(1)} %bitcast.33), channel_id=6, replica_groups=mesh['row_0'=4,'row_1'=4,'col'=16] {'row_0'}, dimensions={0}, use_global_device_ids=true | all-gather | bytes 2560 | tf_op jit(solution)/shard_map/all_gather | solution.py:13
  179.7 8.1 %all-gather.21 = f32[4,1,128]{2,1,0:T(1,128)S(1)} all-gather(f32[1,1,128]{2,1,0:T(1,128)S(1)} %bitcast.36), channel_id=7, replica_groups=mesh['row_0'=4,'row_1'=4,'col'=16] {'row_1'}, dimensions={0}, use_global_device_ids=true | all-gather | bytes 2560 | tf_op jit(solution)/shard_map/all_gather | solution.py:13
  187.9 7.0 %all-gather.24 = f32[4,1,128]{2,1,0:T(1,128)S(1)} all-gather(f32[1,1,128]{2,1,0:T(1,128)S(1)} %bitcast.32), channel_id=10, replica_groups=mesh['row_0'=4,'row_1'=4,'col'=16] {'row_0'}, dimensions={0}, use_global_device_ids=true | all-gather | bytes 2560 | tf_op jit(solution)/shard_map/all_gather | solution.py:13
  194.9 9.0 %all-gather.25 = f32[4,1,128]{2,1,0:T(1,128)S(1)} all-gather(f32[1,1,128]{2,1,0:T(1,128)S(1)} %bitcast.37), channel_id=11, replica_groups=mesh['row_0'=4,'row_1'=4,'col'=16] {'row_1'}, dimensions={0}, use_global_device_ids=true | all-gather | bytes 2560 | tf_op jit(solution)/shard_map/all_gather | solution.py:13
  203.9 7.8 %all-gather.28 = f32[4,1,128]{2,1,0:T(1,128)S(1)} all-gather(f32[1,1,128]{2,1,0:T(1,128)S(1)} %bitcast.31), channel_id=14, replica_groups=mesh['row_0'=4,'row_1'=4,'col'=16] {'row_0'}, dimensions={0}, use_global_device_ids=true | all-gather | bytes 2560 | tf_op jit(solution)/shard_map/all_gather | solution.py:13
  211.7 8.1 %all-gather.29 = f32[4,1,128]{2,1,0:T(1,128)S(1)} all-gather(f32[1,1,128]{2,1,0:T(1,128)S(1)} %bitcast.38), channel_id=15, replica_groups=mesh['row_0'=4,'row_1'=4,'col'=16] {'row_1'}, dimensions={0}, use_global_device_ids=true | all-gather | bytes 2560 | tf_op jit(solution)/shard_map/all_gather | solution.py:13
  219.9 0.2 fusion
  220.0 7.0 %all-gather.30 = f32[4,1,128]{2,1,0:T(1,128)S(1)} all-gather(f32[1,1,128]{2,1,0:T(1,128)S(1)} %bitcast.46), channel_id=16, replica_groups=mesh['row_0'=4,'row_1'=4,'col'=16] {'row_0'}, dimensions={0}, use_global_device_ids=true | all-gather | bytes 2560 | tf_op jit(solution)/shard_map/all_gather | solution.py:13
  227.1 9.0 %all-gather.31 = f32[4,1,128]{2,1,0:T(1,128)S(1)} all-gather(f32[1,1,128]{2,1,0:T(1,128)S(1)} %bitcast.39), channel_id=17, replica_groups=mesh['row_0'=4,'row_1'=4,'col'=16] {'row_1'}, dimensions={0}, use_global_device_ids=true | all-gather | bytes 2560 | tf_op jit(solution)/shard_map/all_gather | solution.py:13
  236.1 7.8 %all-gather.26 = f32[4,1,128]{2,1,0:T(1,128)S(1)} all-gather(f32[1,1,128]{2,1,0:T(1,128)S(1)} %bitcast.45), channel_id=12, replica_groups=mesh['row_0'=4,'row_1'=4,'col'=16] {'row_0'}, dimensions={0}, use_global_device_ids=true | all-gather | bytes 2560 | tf_op jit(solution)/shard_map/all_gather | solution.py:13
  243.9 8.1 %all-gather.27 = f32[4,1,128]{2,1,0:T(1,128)S(1)} all-gather(f32[1,1,128]{2,1,0:T(1,128)S(1)} %bitcast.40), channel_id=13, replica_groups=mesh['row_0'=4,'row_1'=4,'col'=16] {'row_1'}, dimensions={0}, use_global_device_ids=true | all-gather | bytes 2560 | tf_op jit(solution)/shard_map/all_gather | solution.py:13
  252.1 7.0 %all-gather.22 = f32[4,1,128]{2,1,0:T(1,128)S(1)} all-gather(f32[1,1,128]{2,1,0:T(1,128)S(1)} %bitcast.44), channel_id=8, replica_groups=mesh['row_0'=4,'row_1'=4,'col'=16] {'row_0'}, dimensions={0}, use_global_device_ids=true | all-gather | bytes 2560 | tf_op jit(solution)/shard_map/all_gather | solution.py:13
  259.1 9.0 %all-gather.23 = f32[4,1,128]{2,1,0:T(1,128)S(1)} all-gather(f32[1,1,128]{2,1,0:T(1,128)S(1)} %bitcast.41), channel_id=9, replica_groups=mesh['row_0'=4,'row_1'=4,'col'=16] {'row_1'}, dimensions={0}, use_global_device_ids=true | all-gather | bytes 2560 | tf_op jit(solution)/shard_map/all_gather | solution.py:13
  268.1 7.8 %all-gather.18 = f32[4,1,128]{2,1,0:T(1,128)S(1)} all-gather(f32[1,1,128]{2,1,0:T(1,128)S(1)} %bitcast.43), channel_id=4, replica_groups=mesh['row_0'=4,'row_1'=4,'col'=16] {'row_0'}, dimensions={0}, use_global_device_ids=true | all-gather | bytes 2560 | tf_op jit(solution)/shard_map/all_gather | solution.py:13
  275.9 8.1 %all-gather.19 = f32[4,1,128]{2,1,0:T(1,128)S(1)} all-gather(f32[1,1,128]{2,1,0:T(1,128)S(1)} %bitcast.42), channel_id=5, replica_groups=mesh['row_0'=4,'row_1'=4,'col'=16] {'row_1'}, dimensions={0}, use_global_device_ids=true | all-gather | bytes 2560 | tf_op jit(solution)/shard_map/all_gather | solution.py:13
  284.1 0.2 divide_convert_fusion.3
  284.3 0.9 pad_maximum_fusion
  (21 shorter events, 0.4 us)
Async XLA Ops:
  6.5 61.8 %all-gather.35.cloned.1.call-start = ((), (), s32[]{:S(2)}) async-start(), calls=%async_computation | async-start | bytes 8912896 | tf_op jit(solution)/shard_map/all_gather | solution.py:33
  9.4 135.8 %all-gather.37.cloned.1.call-start = ((), (), s32[]{:S(2)}) async-start(), calls=%async_computation.1 | async-start | bytes 8912896 | tf_op jit(solution)/shard_map/all_gather | solution.py:31
Sparse Core Ops, SparseCore 0:
  9.5 58.7 all-gather.34
  70.7 74.3 all-gather.36
